TPU v7x, 32 devices: a whole 2x2x4 slice. The times are simulated.
32 devices in a mesh: seq: 8 (over z, x), mp: 4 (over y, core).
Axes of the slice: x: 2, y: 2, z: 4, core: 2. Of those that a mesh axis runs over, the one named last changes fastest.
Arguments:
- grad_rows: bfloat16 [4096, 8192], P('seq', 'mp'), may hold values from -6 to 6
- img_start: int32 [64], replicated, may hold values from 0 to 4092, as said below
- img_len: int32 [64], replicated, may hold values from 4 to 64, as said below
- img_owner: int32 [64], replicated, may hold values from 0 to 7, as said below
- pre_act: bfloat16 [4096, 5120], P('seq', 'mp'), may hold values from -6 to 6
- w_out: bfloat16 [5120, 8192], P(None, 'mp'), may hold values from -0.0625 to 0.0625
Outputs:
- pre_grad: bfloat16 [4096, 5120], P('seq', 'mp')
- weight_grad: bfloat16 [5120, 8192], P('seq', 'mp')
Inputs may be any that keep to these rules, and one draw needn't show every extreme that they name: Image i lies inside positions i * 64 to (i + 1) * 64 - 1: img_start[i] - i * 64 + img_len[i] <= 64. `img_len`: A multiple of 4. In every draw some owner has all its images of exactly 64 merged tokens. `img_owner`: the images i with one value of i % 8 all have different owners, and so do the 8 images of one stripe (images i with one value of i // 8).
All inputs are finite; a program needn't handle non-finite values.
Results may differ from a plain program's by a relative error of at most 0.02.
Values may be sent and summed in bfloat16 or wider, within the bound.
A program may use at most 192 MiB of HBM per device.

v0:
```python
import math
import jax
import jax.numpy as jnp
from jax import lax
from jax.sharding import PartitionSpec as P

FRAME = 64


def gelu_parts(values):
    normal_cdf = 0.5 * (1.0 + lax.erf(values * 0.7071067811865476))
    density = jnp.exp(-0.5 * values * values) * 0.3989422804014327
    return (values * normal_cdf, normal_cdf + values * density)


def local(grad_rows, img_start, img_len, img_owner, pre_act, w_out):
    stripe = grad_rows.shape[0]
    quarter = grad_rows.shape[1]
    frames = stripe // FRAME
    owners_total = lax.axis_size("seq")
    here = lax.axis_index("seq")
    within = jnp.arange(FRAME, dtype=jnp.int32)
    first_image = here * frames
    starts = lax.dynamic_slice_in_dim(img_start, first_image, frames)
    lengths = lax.dynamic_slice_in_dim(img_len, first_image, frames)
    my_owners = lax.dynamic_slice_in_dim(img_owner, first_image, frames)
    offsets = starts - here * stripe
    row_ids = jnp.clip(offsets[:, None] + within[None, :], 0, stripe - 1)
    filled = within[None, :] < lengths[:, None]
    blocks = jnp.where(filled[:, :, None], grad_rows[row_ids], jnp.zeros((), jnp.bfloat16))
    owner_ids = jnp.arange(owners_total, dtype=jnp.int32)
    placing = (my_owners[None, :] == owner_ids[:, None]).astype(jnp.bfloat16)
    outgoing = jnp.dot(
        placing, blocks.reshape(frames, FRAME * quarter), preferred_element_type=jnp.float32
    )
    outgoing = outgoing.astype(jnp.bfloat16).reshape(owners_total * FRAME, quarter)
    received = lax.all_to_all(outgoing, "seq", split_axis=0, concat_axis=0, tiled=True)
    choosing = (img_owner.reshape(owners_total, frames) == here).T.astype(jnp.bfloat16)
    routed = jnp.dot(
        choosing,
        received.reshape(owners_total, FRAME * quarter),
        preferred_element_type=jnp.float32,
    )
    routed = routed.astype(jnp.bfloat16).reshape(stripe, quarter)
    hidden_terms = lax.dot_general(
        routed, w_out, (((1,), (1,)), ((), ())), preferred_element_type=jnp.float32
    )
    hidden_grad = lax.psum_scatter(
        hidden_terms.astype(jnp.bfloat16), "mp", scatter_dimension=1, tiled=True
    ).astype(jnp.float32)
    _, derivative = gelu_parts(pre_act.astype(jnp.float32))
    pre_grad = (hidden_grad * derivative).astype(jnp.bfloat16)
    pre_full = lax.all_gather(pre_act, "mp", axis=1, tiled=True)
    activation, _ = gelu_parts(pre_full.astype(jnp.float32))
    activation = activation.astype(jnp.bfloat16)
    factor = 1.0 / math.sqrt(owners_total * stripe)
    kept_rows = activation.shape[1] // owners_total
    act_columns = lax.all_to_all(activation, "seq", split_axis=1, concat_axis=0, tiled=True)
    shard_rows = lax.all_gather(routed, "seq", axis=0, tiled=True)
    owners_here = shard_rows.shape[0] // stripe
    product = (
        jnp.einsum(
            "kar,kaq->krq",
            act_columns.reshape(owners_here, stripe, kept_rows),
            shard_rows.reshape(owners_here, stripe, quarter),
            preferred_element_type=jnp.float32,
        )
        * factor
    )
    product = lax.optimization_barrier(product.astype(jnp.bfloat16))
    weight_grad = jnp.sum(product.astype(jnp.float32), axis=0)
    return (pre_grad, weight_grad.astype(jnp.bfloat16))


def solution(mesh):
    return jax.shard_map(
        local,
        mesh=mesh,
        in_specs=(P("seq", "mp"), P(), P(), P(), P("seq", "mp"), P(None, "mp")),
        out_specs=(P("seq", "mp"), P("seq", "mp")),
        check_vma=False,
    )
```

profile of v0, /device:TPU:0, one launch (start us, length us, event | category | flops | bytes accessed | tf_op | source)
XLA Modules:
  0.0 487.9 jit_solution(11134335510358859104)
XLA Ops:
  7.2 0.7 all-gather.3.cloned.1.call-update
  7.9 0.7 dynamic-slice_subtract_fusion
  8.8 0.7 dynamic_slice.10
  9.6 3.3 gather_fusion
  12.9 1.8 select_bitcast_fusion
  14.7 1.2 copy.12
  16.0 0.7 convolution_convert_fusion.1
  16.7 2.5 copy.10
  19.1 7.3 %all-to-all-start = ((bf16[8,64,2048]{2,1,0:T(8,128)(2,1)}), bf16[8,64,2048]{2,1,0:T(8,128)(2,1)S(1)}, u32[]{:S(2)}, u32[]{:S(2)}) async-start(bf16[8,64,2048]{2,1,0:T(8,128)(2,1)} %copy.10), calls=%async_computation | async-start | bytes 4194304 | tf_op jit(solution)/shard_map/all_to_all | solution.py:37
  26.7 47.9 %all-to-all-done = bf16[8,64,2048]{2,1,0:T(8,128)(2,1)S(1)} async-done(((bf16[8,64,2048]{2,1,0:T(8,128)(2,1)}), bf16[8,64,2048]{2,1,0:T(8,128)(2,1)S(1)}, u32[]{:S(2)}, u32[]{:S(2)}) %all-to-all-start) | async-done | bytes 2097184 | tf_op jit(solution)/shard_map/all_to_all | solution.py:37
  74.7 1.3 copy-done.3
  76.0 2.7 copy.13
  78.7 2.0 convolution_convert_fusion
  80.7 2.5 reshape.96
  83.2 17.5 %convolution_convert_fusion.2 = bf16[512,5120]{1,0:T(8,128)(2,1)} fusion(bf16[512,2048]{1,0:T(8,128)(2,1)S(1)} %reshape.96, bf16[5120,2048]{1,0:T(8,128)(2,1)} %param.11), kind=kOutput, calls=%fused_computation.10 | convolution fusion | flops 10740039680 | bytes 28311552 | tf_op jit(solution)/shard_map/dot_general | solution.py:45
  101.5 6.6 %fusion.3 = bf16[512,5120]{1,0:T(8,128)(2,1)} fusion(bf16[512,5120]{1,0:T(8,128)(2,1)} %all-gather.3.cloned.1.call-done), kind=kLoop, calls=%fused_computation.9 | loop fusion | flops 15728640 | bytes 10485760 | tf_op jit(solution)/shard_map/convert_element_type | solution.py:55
  108.1 7.7 %copy.11 = bf16[512,5120]{0,1:T(8,128)(2,1)} copy(bf16[512,5120]{1,0:T(8,128)(2,1)} %fusion.3) | data formatting | bytes 10485760 | tf_op jit(solution)/shard_map/convert_element_type | solution.py:55
  115.9 5.0 %all-to-all-start.1 = ((bf16[512,8,640]{0,2,1:T(8,128)(2,1)}), bf16[512,8,640]{0,2,1:T(8,128)(2,1)}, u32[]{:S(2)}, u32[]{:S(2)}) async-start(bf16[512,8,640]{0,2,1:T(8,128)(2,1)} %bitcast.20), calls=%async_computation.2 | async-start | bytes 10485760 | tf_op jit(solution)/shard_map/all_to_all | solution.py:58
  120.9 30.3 %reduce-scatter.2.cloned.1.call-done = bf16[512,1280]{1,0:T(8,128)(2,1)} async-done(((bf16[512,5120]{1,0:T(8,128)(2,1)}), bf16[512,1280]{1,0:T(8,128)(2,1)}) %reduce-scatter.2.cloned.1.call-update) | async-done | bytes 1310736 | tf_op jit(solution)/shard_map/reduce_scatter | solution.py:48
  151.2 3.2 fusion.12
  154.4 144.3 %all-to-all-done.1 = bf16[512,8,640]{0,2,1:T(8,128)(2,1)} async-done(((bf16[512,8,640]{0,2,1:T(8,128)(2,1)}), bf16[512,8,640]{0,2,1:T(8,128)(2,1)}, u32[]{:S(2)}, u32[]{:S(2)}) %all-to-all-start.1) | async-done | bytes 5242912 | tf_op jit(solution)/shard_map/all_to_all | solution.py:58
  298.7 148.5 %all-gather.5.cloned.1.call-done = bf16[4096,2048]{1,0:T(8,128)(2,1)} async-done(((bf16[512,2048]{1,0:T(8,128)(2,1)}), bf16[4096,2048]{1,0:T(8,128)(2,1)}) %all-gather.5.cloned.1.call-update) | async-done | bytes 16777232 | tf_op jit(solution)/shard_map/all_gather | solution.py:59
  447.2 20.8 %multiply_convert_fusion = bf16[8,640,2048]{2,1,0:T(8,128)(2,1)} fusion(bf16[8,512,2048]{2,1,0:T(8,128)(2,1)} %bitcast.26, bf16[512,8,640]{0,2,1:T(8,128)(2,1)} %all-to-all-done.1), kind=kOutput, calls=%fused_computation.3 | convolution fusion | flops 10758389760 | bytes 42991616 | tf_op jit(solution)/shard_map/kar,kaq->krq/dot_general | solution.py:62
  468.0 13.4 %reduce_sum.12 = bf16[640,2048]{1,0:T(8,128)(2,1)} reduce(bf16[8,640,2048]{2,1,0:T(8,128)(2,1)} %multiply_convert_fusion, bf16[]{:T(256)} %constant.4.clone.1), dimensions={0}, to_apply=%region_1.2 | reduce | flops 9175040 | bytes 23592962 | tf_op jit(solution)/shard_map/reduce_sum | solution.py:71
  (24 shorter events, 1.4 us)
Async XLA Ops:
  7.2 2.4 copy-start
  7.2 94.3 %all-gather.3.cloned.1.call-start = ((), (), s32[]{:S(2)}) async-start(), calls=%async_computation.4 | async-start | bytes 6553600 | tf_op jit(solution)/shard_map/all_gather | solution.py:53
  14.7 1.2 copy-start.5
  19.1 55.5 %all-to-all-start = ((bf16[8,64,2048]{2,1,0:T(8,128)(2,1)}), bf16[8,64,2048]{2,1,0:T(8,128)(2,1)S(1)}, u32[]{:S(2)}, u32[]{:S(2)}) async-start(bf16[8,64,2048]{2,1,0:T(8,128)(2,1)} %copy.10), calls=%async_computation | async-start | bytes 4194304 | tf_op jit(solution)/shard_map/all_to_all | solution.py:37
  26.4 124.8 %reduce-scatter.2.cloned.1.call-start = ((), (), s32[]{:S(2)}) async-start(), calls=%async_computation.3 | async-start | bytes 6553600 | tf_op jit(solution)/shard_map/reduce_scatter | solution.py:48
  74.7 1.3 copy-start.3
  83.2 17.5 %copy-start.2 = (bf16[512,2048]{1,0:T(8,128)(2,1)}, bf16[512,2048]{1,0:T(8,128)(2,1)S(1)}, u32[]{:S(2)}) copy-start(bf16[512,2048]{1,0:T(8,128)(2,1)S(1)} %reshape.96) | copy-start | bytes 6291460
  100.8 346.4 %all-gather.5.cloned.1.call-start = ((), (), s32[]{:S(2)}) async-start(), calls=%async_computation.5 | async-start | bytes 18874368 | tf_op jit(solution)/shard_map/all_gather | solution.py:59
  115.9 35.3 %copy-start.4 = (bf16[512,1280]{1,0:T(8,128)(2,1)S(1)}, bf16[512,1280]{1,0:T(8,128)(2,1)}, u32[]{:S(2)}) copy-start(bf16[512,1280]{1,0:T(8,128)(2,1)} %param.10) | copy-start | bytes 3932164
  115.9 182.8 %all-to-all-start.1 = ((bf16[512,8,640]{0,2,1:T(8,128)(2,1)}), bf16[512,8,640]{0,2,1:T(8,128)(2,1)}, u32[]{:S(2)}, u32[]{:S(2)}) async-start(bf16[512,8,640]{0,2,1:T(8,128)(2,1)} %bitcast.20), calls=%async_computation.2 | async-start | bytes 10485760 | tf_op jit(solution)/shard_map/all_to_all | solution.py:58
  468.0 13.4 %copy-start.1 = (bf16[512,2048]{1,0:T(8,128)(2,1)S(1)}, bf16[512,2048]{1,0:T(8,128)(2,1)}, u32[]{:S(2)}) copy-start(bf16[512,2048]{1,0:T(8,128)(2,1)} %param.6) | copy-start | bytes 6291460
Sparse Core Ops, SparseCore 0:
  9.5 43.1 all-gather.2
  100.9 50.2 reduce-scatter.1
  153.9 293.2 all-gather.4
where the time goes:
time: 489 us; the launch traced here: 488 us
  waiting for transfers between devices  372 us (76%)
  matrix products  40.9 us (8%)
  other arithmetic  25.8 us (5%)
  local copies, waits for them, and re-layouts  22.3 us (5%)
  between operations  13.8 us (3%)
  starting transfers between devices  12.6 us (3%)
    all_gather x1, waiting for transfers between devices, local(): shard_rows = lax.all_gather(routed, 'seq', axis=0, tiled=True)  148 us
    all_to_all x1, waiting for transfers between devices, local(): lax.all_to_all(activation, 'seq', split_axis=1, concat_axis=0, tiled=True)  144 us
    all_to_all x1, waiting for transfers between devices, local(): lax.all_to_all(outgoing, 'seq', split_axis=0, concat_axis=0, tiled=True)  47.9 us
    reduce_scatter x1, waiting for transfers between devices, local(): lax.psum_scatter(hidden_terms.astype(jnp.bfloat16), 'mp', scatter_dimensi...  30.3 us
    dot_general x1, matrix products, local(): jnp.einsum('kar,kaq->krq', act_columns.reshape(owners_here, stripe, kept_...  20.8 us
    dot_general x1, matrix products, local(): lax.dot_general(routed, w_out, (((1,), (1,)), ((), ())), preferred_elemen...  17.5 us
    reduce_sum x1, other arithmetic, local(): weight_grad = jnp.sum(product.astype(jnp.float32), axis=0)  13.4 us
  transfers between devices with their start and end apart: 5, of which 4 were waited for; matrix products, arithmetic and copies ran while one was open for 11% of the time, Pallas kernels for 0%

commit v1 on v0

--- a/solution.py
+++ b/solution.py
@@ -56,7 +56,21 @@
     factor = 1.0 / math.sqrt(owners_total * stripe)
     kept_rows = activation.shape[1] // owners_total
     act_columns = lax.all_to_all(activation, "seq", split_axis=1, concat_axis=0, tiled=True)
-    shard_rows = lax.all_gather(routed, "seq", axis=0, tiled=True)
+
+    def do_the_points(t0):
+        degree = lax.axis_size("seq")
+        queue = [t0]
+        num = 0
+        while num < degree - 1:
+            queue.append(
+                lax.ppermute(queue[-1], "seq", [(k, (k + 1) % degree) for k in range(degree)])
+            )
+            num += 1
+        return jnp.roll(
+            jnp.concatenate(queue[::-1], 0), (lax.axis_index("seq") + 1) * t0.shape[0], 0
+        )
+
+    shard_rows = do_the_points(routed)
     owners_here = shard_rows.shape[0] // stripe
     product = (
         jnp.einsum(

time: 489 us -> 584 us (1.19)
  the two profiles are of different devices: /device:TPU:0 before, /device:TPU:16 now
where the time goes in v1:
time: 584 us; the launch traced here: 583 us
  waiting for transfers between devices  415 us (71%)
  local copies, waits for them, and re-layouts  50.9 us (9%)
  matrix products  40.2 us (7%)
  starting transfers between devices  36.6 us (6%)
  other arithmetic  25.7 us (4%)
  between operations  14.2 us (2%)
    ppermute x7, waiting for transfers between devices, do_the_points(): lax.ppermute(queue[-1], 'seq', [(k, (k + 1) % degree) for k in range(degr...  370 us
    all_to_all x1, waiting for transfers between devices, local(): lax.all_to_all(outgoing, 'seq', split_axis=0, concat_axis=0, tiled=True)  44.1 us
    unnamed x35, local copies, waits for them, and re-layouts  26.8 us
    dot_general x1, matrix products, local(): jnp.einsum('kar,kaq->krq', act_columns.reshape(owners_here, stripe, kept_...  20.7 us
    ppermute x7, starting transfers between devices, do_the_points(): lax.ppermute(queue[-1], 'seq', [(k, (k + 1) % degree) for k in range(degr...  20 us
    dot_general x1, matrix products, local(): lax.dot_general(routed, w_out, (((1,), (1,)), ((), ())), preferred_elemen...  16.8 us
    reduce_sum x1, other arithmetic, local(): weight_grad = jnp.sum(product.astype(jnp.float32), axis=0)  13.4 us
  transfers between devices with their start and end apart: 11, of which 8 were waited for; matrix products, arithmetic and copies ran while one was open for 12% of the time, Pallas kernels for 0%

profile of v1, /device:TPU:16, one launch (start us, length us, event | category | flops | bytes accessed | tf_op | source)
XLA Modules:
  0.0 582.6 jit_solution(10587824623787970456)
XLA Ops:
  9.0 3.3 gather_fusion
  18.6 6.1 %all-to-all-start = ((bf16[8,64,2048]{2,1,0:T(8,128)(2,1)}), bf16[8,64,2048]{2,1,0:T(8,128)(2,1)S(1)}, u32[]{:S(2)}, u32[]{:S(2)}) async-start(bf16[8,64,2048]{2,1,0:T(8,128)(2,1)} %copy.10), calls=%async_computation | async-start | bytes 4194304 | tf_op jit(solution)/shard_map/all_to_all | solution.py:37
  25.6 44.1 %all-to-all-done = bf16[8,64,2048]{2,1,0:T(8,128)(2,1)S(1)} async-done(((bf16[8,64,2048]{2,1,0:T(8,128)(2,1)}), bf16[8,64,2048]{2,1,0:T(8,128)(2,1)S(1)}, u32[]{:S(2)}, u32[]{:S(2)}) %all-to-all-start) | async-done | bytes 2097184 | tf_op jit(solution)/shard_map/all_to_all | solution.py:37
  71.0 2.7 copy.13
  79.7 45.9 %collective-permute-done = bf16[512,2048]{1,0:T(8,128)(2,1)} collective-permute-done((bf16[512,2048]{1,0:T(8,128)(2,1)S(1)}, bf16[512,2048]{1,0:T(8,128)(2,1)}, u32[]{:S(2)}, u32[]{:S(2)}) %collective-permute-start) | collective-permute-done | bytes 2097184 | tf_op jit(solution)/shard_map/ppermute | solution.py:66
  128.0 16.8 %convolution_convert_fusion.2 = bf16[512,5120]{1,0:T(8,128)(2,1)} fusion(bf16[512,2048]{1,0:T(8,128)(2,1)S(1)} %reshape.96, bf16[5120,2048]{1,0:T(8,128)(2,1)} %param.11), kind=kOutput, calls=%fused_computation.10 | convolution fusion | flops 10740039680 | bytes 28311552 | tf_op jit(solution)/shard_map/dot_general | solution.py:45
  144.8 27.9 %collective-permute-done.1 = bf16[512,2048]{1,0:T(8,128)(2,1)} collective-permute-done((bf16[512,2048]{1,0:T(8,128)(2,1)}, bf16[512,2048]{1,0:T(8,128)(2,1)}, u32[]{:S(2)}, u32[]{:S(2)}) %collective-permute-start.1) | collective-permute-done | bytes 2097184 | tf_op jit(solution)/shard_map/ppermute | solution.py:66
  172.7 3.3 collective-permute-start.2
  176.0 43.7 %collective-permute-done.2 = bf16[512,2048]{1,0:T(8,128)(2,1)S(1)} collective-permute-done((bf16[512,2048]{1,0:T(8,128)(2,1)}, bf16[512,2048]{1,0:T(8,128)(2,1)S(1)}, u32[]{:S(2)}, u32[]{:S(2)}) %collective-permute-start.2) | collective-permute-done | bytes 2097184 | tf_op jit(solution)/shard_map/ppermute | solution.py:66
  221.1 3.4 collective-permute-start.3
  224.5 42.5 %collective-permute-done.3 = bf16[512,2048]{1,0:T(8,128)(2,1)S(1)} collective-permute-done((bf16[512,2048]{1,0:T(8,128)(2,1)S(1)}, bf16[512,2048]{1,0:T(8,128)(2,1)S(1)}, u32[]{:S(2)}, u32[]{:S(2)}) %collective-permute-start.3) | collective-permute-done | bytes 2097184 | tf_op jit(solution)/shard_map/ppermute | solution.py:66
  268.3 3.3 collective-permute-start.4
  271.6 42.3 %collective-permute-done.4 = bf16[512,2048]{1,0:T(8,128)(2,1)} collective-permute-done((bf16[512,2048]{1,0:T(8,128)(2,1)S(1)}, bf16[512,2048]{1,0:T(8,128)(2,1)}, u32[]{:S(2)}, u32[]{:S(2)}) %collective-permute-start.4) | collective-permute-done | bytes 2097184 | tf_op jit(solution)/shard_map/ppermute | solution.py:66
  313.9 3.2 collective-permute-start.5
  317.1 6.3 %fusion.3 = bf16[512,5120]{1,0:T(8,128)(2,1)} fusion(bf16[512,5120]{1,0:T(8,128)(2,1)} %all-gather.2.cloned.1.call-done), kind=kLoop, calls=%fused_computation.9 | loop fusion | flops 15728640 | bytes 10485760 | tf_op jit(solution)/shard_map/convert_element_type | solution.py:55
  323.4 7.9 %copy.11 = bf16[512,5120]{0,1:T(8,128)(2,1)} copy(bf16[512,5120]{1,0:T(8,128)(2,1)} %fusion.3) | data formatting | bytes 10485760 | tf_op jit(solution)/shard_map/convert_element_type | solution.py:55
  331.3 10.4 %all-to-all-start.1 = ((bf16[512,8,640]{0,2,1:T(8,128)(2,1)}), bf16[512,8,640]{0,2,1:T(8,128)(2,1)}, u32[]{:S(2)}, u32[]{:S(2)}) async-start(bf16[512,8,640]{0,2,1:T(8,128)(2,1)} %bitcast.20), calls=%async_computation.2 | async-start | bytes 10485760 | tf_op jit(solution)/shard_map/all_to_all | solution.py:58
  341.7 55.5 %collective-permute-done.5 = bf16[512,2048]{1,0:T(8,128)(2,1)} collective-permute-done((bf16[512,2048]{1,0:T(8,128)(2,1)}, bf16[512,2048]{1,0:T(8,128)(2,1)}, u32[]{:S(2)}, u32[]{:S(2)}) %collective-permute-start.5) | collective-permute-done | bytes 2097184 | tf_op jit(solution)/shard_map/ppermute | solution.py:66
  397.2 3.0 collective-permute-start.6
  400.2 3.2 fusion.12
  403.4 112.4 %collective-permute-done.6 = bf16[512,2048]{1,0:T(8,128)(2,1)} collective-permute-done((bf16[512,2048]{1,0:T(8,128)(2,1)}, bf16[512,2048]{1,0:T(8,128)(2,1)}, u32[]{:S(2)}, u32[]{:S(2)}) %collective-permute-start.6) | collective-permute-done | bytes 2097184 | tf_op jit(solution)/shard_map/ppermute | solution.py:66
  534.9 6.7 %constant_dynamic-slice_fusion = bf16[4096,2048]{1,0:T(8,128)(2,1)} fusion(bf16[8192,2048]{1,0:T(8,128)(2,1)S(1)} %constant_dynamic-update-slice_fusion, s32[]{:T(128)S(6)} %select_n.41), kind=kLoop, calls=%fused_computation.47 | loop fusion | bytes 33554436 | tf_op jit(solution)/shard_map/jit(_roll_dynamic)/dynamic_slice | solution.py:69
  541.6 20.7 %multiply_convert_fusion = bf16[8,640,2048]{2,1,0:T(8,128)(2,1)} fusion(bf16[8,512,2048]{2,1,0:T(8,128)(2,1)} %bitcast.21, bf16[512,8,640]{0,2,1:T(8,128)(2,1)} %all-to-all-done.1), kind=kOutput, calls=%fused_computation.3 | convolution fusion | flops 10758389760 | bytes 42991616 | tf_op jit(solution)/shard_map/kar,kaq->krq/dot_general | solution.py:76
  562.4 13.4 %reduce_sum.12 = bf16[640,2048]{1,0:T(8,128)(2,1)} reduce(bf16[8,640,2048]{2,1,0:T(8,128)(2,1)} %multiply_convert_fusion, bf16[]{:T(256)} %constant.25.clone.1), dimensions={0}, to_apply=%region_1.2 | reduce | flops 9175040 | bytes 23592962 | tf_op jit(solution)/shard_map/reduce_sum | solution.py:85
  (58 shorter events, 40.3 us)
Async XLA Ops:
  7.2 1.9 copy-start
  12.3 3.0 copy-start.8
  18.6 51.1 %all-to-all-start = ((bf16[8,64,2048]{2,1,0:T(8,128)(2,1)}), bf16[8,64,2048]{2,1,0:T(8,128)(2,1)S(1)}, u32[]{:S(2)}, u32[]{:S(2)}) async-start(bf16[8,64,2048]{2,1,0:T(8,128)(2,1)} %copy.10), calls=%async_computation | async-start | bytes 4194304 | tf_op jit(solution)/shard_map/all_to_all | solution.py:37
  24.7 292.4 %all-gather.2.cloned.1.call-start = ((), (), s32[]{:S(2)}) async-start(), calls=%async_computation.4 | async-start | bytes 6553600 | tf_op jit(solution)/shard_map/all_gather | solution.py:53
  25.4 374.8 %reduce-scatter.2.cloned.1.call-start = ((), (), s32[]{:S(2)}) async-start(), calls=%async_computation.3 | async-start | bytes 6553600 | tf_op jit(solution)/shard_map/reduce_scatter | solution.py:48
  69.7 1.3 copy-start.6
  78.2 47.4 %collective-permute-start = (bf16[512,2048]{1,0:T(8,128)(2,1)S(1)}, bf16[512,2048]{1,0:T(8,128)(2,1)}, u32[]{:S(2)}, u32[]{:S(2)}) collective-permute-start(bf16[512,2048]{1,0:T(8,128)(2,1)S(1)} %reshape.96), channel_id=1, source_target_pairs={{0,4},{4,8},{8,12},{12,16},{16,20},{20,24},{24,28},{28,0},{1,5},{5... | collective-permute-start | bytes 6291464 | tf_op jit(solution)/shard_map/ppermute | solution.py:66
  125.7 47.0 %collective-permute-start.1 = (bf16[512,2048]{1,0:T(8,128)(2,1)}, bf16[512,2048]{1,0:T(8,128)(2,1)}, u32[]{:S(2)}, u32[]{:S(2)}) collective-permute-start(bf16[512,2048]{1,0:T(8,128)(2,1)} %collective-permute-done), channel_id=1, source_target_pairs={{0,4},{4,8},{8,12},{12,16},{16,20},{20,24},{24,28},{28,0},{1,5},{5... | collective-permute-start | bytes 6291464 | tf_op jit(solution)/shard_map/ppermute | solution.py:66
  172.7 47.0 %collective-permute-start.2 = (bf16[512,2048]{1,0:T(8,128)(2,1)}, bf16[512,2048]{1,0:T(8,128)(2,1)S(1)}, u32[]{:S(2)}, u32[]{:S(2)}) collective-permute-start(bf16[512,2048]{1,0:T(8,128)(2,1)} %collective-permute-done.1), channel_id=1, source_target_pairs={{0,4},{4,8},{8,12},{12,16},{16,20},{20,24},{24,28},{28,0},{1,5},{5... | collective-permute-start | bytes 6291464 | tf_op jit(solution)/shard_map/ppermute | solution.py:66
  219.7 1.4 copy-start.2
  221.1 45.9 %collective-permute-start.3 = (bf16[512,2048]{1,0:T(8,128)(2,1)S(1)}, bf16[512,2048]{1,0:T(8,128)(2,1)S(1)}, u32[]{:S(2)}, u32[]{:S(2)}) collective-permute-start(bf16[512,2048]{1,0:T(8,128)(2,1)S(1)} %collective-permute-done.2), channel_id=1, source_target_pairs={{0,4},{4,8},{8,12},{12,16},{16,20},{20,24},{24,28},{28,0},{1,5},{5... | collective-permute-start | bytes 6291464 | tf_op jit(solution)/shard_map/ppermute | solution.py:66
  267.0 1.3 copy-start.4
  268.3 45.6 %collective-permute-start.4 = (bf16[512,2048]{1,0:T(8,128)(2,1)S(1)}, bf16[512,2048]{1,0:T(8,128)(2,1)}, u32[]{:S(2)}, u32[]{:S(2)}) collective-permute-start(bf16[512,2048]{1,0:T(8,128)(2,1)S(1)} %collective-permute-done.3), channel_id=1, source_target_pairs={{0,4},{4,8},{8,12},{12,16},{16,20},{20,24},{24,28},{28,0},{1,5},{5... | collective-permute-start | bytes 6291464 | tf_op jit(solution)/shard_map/ppermute | solution.py:66
  313.9 83.3 %collective-permute-start.5 = (bf16[512,2048]{1,0:T(8,128)(2,1)}, bf16[512,2048]{1,0:T(8,128)(2,1)}, u32[]{:S(2)}, u32[]{:S(2)}) collective-permute-start(bf16[512,2048]{1,0:T(8,128)(2,1)} %collective-permute-done.4), channel_id=1, source_target_pairs={{0,4},{4,8},{8,12},{12,16},{16,20},{20,24},{24,28},{28,0},{1,5},{5... | collective-permute-start | bytes 6291464 | tf_op jit(solution)/shard_map/ppermute | solution.py:66
  331.3 68.9 %copy-start.7 = (bf16[512,1280]{1,0:T(8,128)(2,1)S(1)}, bf16[512,1280]{1,0:T(8,128)(2,1)}, u32[]{:S(2)}) copy-start(bf16[512,1280]{1,0:T(8,128)(2,1)} %param.10) | copy-start | bytes 3932164
  331.3 210.3 %all-to-all-start.1 = ((bf16[512,8,640]{0,2,1:T(8,128)(2,1)}), bf16[512,8,640]{0,2,1:T(8,128)(2,1)}, u32[]{:S(2)}, u32[]{:S(2)}) async-start(bf16[512,8,640]{0,2,1:T(8,128)(2,1)} %bitcast.20), calls=%async_computation.2 | async-start | bytes 10485760 | tf_op jit(solution)/shard_map/all_to_all | solution.py:58
  397.2 118.6 %collective-permute-start.6 = (bf16[512,2048]{1,0:T(8,128)(2,1)}, bf16[512,2048]{1,0:T(8,128)(2,1)}, u32[]{:S(2)}, u32[]{:S(2)}) collective-permute-start(bf16[512,2048]{1,0:T(8,128)(2,1)} %collective-permute-done.5), channel_id=1, source_target_pairs={{0,4},{4,8},{8,12},{12,16},{16,20},{20,24},{24,28},{28,0},{1,5},{5... | collective-permute-start | bytes 6291464 | tf_op jit(solution)/shard_map/ppermute | solution.py:66
  517.5 3.8 copy-start.5
  519.4 2.3 copy-start.3
  562.4 13.4 %copy-start.1 = (bf16[512,2048]{1,0:T(8,128)(2,1)S(1)}, bf16[512,2048]{1,0:T(8,128)(2,1)}, u32[]{:S(2)}) copy-start(bf16[512,2048]{1,0:T(8,128)(2,1)} %param.6) | copy-start | bytes 6291460
Sparse Core Ops, SparseCore 0:
  27.0 41.3 all-gather.1
  144.9 54.7 reduce-scatter.1
